TPU v7x, 32 devices: a 4x4x1 block of a 4x4x8 slice. The times are simulated.
32 devices in a mesh: rep: 2 (over z, core), dp: 16 (over x, y).
Axes of the slice: x: 4, y: 4, z: 1, core: 2. Of those that a mesh axis runs over, the one named last changes fastest.
The devices are a block of a 4x4x8 slice.
Arguments:
- x: bfloat16 [32, 2048, 1024], P(('rep', 'dp')), parts along dimension 0
- dy: bfloat16 [32, 2048, 1024], P(('rep', 'dp')), parts along dimension 0
- w_gate: bfloat16 [2, 1024, 2816], replicated
- w_up: bfloat16 [2, 1024, 2816], replicated
- w_down: bfloat16 [2, 2816, 1024], replicated
- m_w_gate: float32 [2, 1024, 2816], replicated
- m_w_up: float32 [2, 1024, 2816], replicated
- m_w_down: float32 [2, 2816, 1024], replicated
- v_w_gate: float32 [2, 1024, 2816], replicated
- v_w_up: float32 [2, 1024, 2816], replicated
- v_w_down: float32 [2, 2816, 1024], replicated
Outputs:
- output 1: bfloat16 [4, 1024, 2816], P('rep'), parts along dimension 0
- output 2: bfloat16 [4, 1024, 2816], P('rep'), parts along dimension 0
- output 3: bfloat16 [4, 2816, 1024], P('rep'), parts along dimension 0
- output 4: float32 [4, 1024, 2816], P('rep'), parts along dimension 0
- output 5: float32 [4, 1024, 2816], P('rep'), parts along dimension 0
- output 6: float32 [4, 2816, 1024], P('rep'), parts along dimension 0
- output 7: float32 [4, 1024, 2816], P('rep'), parts along dimension 0
- output 8: float32 [4, 1024, 2816], P('rep'), parts along dimension 0
- output 9: float32 [4, 2816, 1024], P('rep'), parts along dimension 0
There are 2 independent parts. A program takes and returns all parts, laid end to end along the dimension named above; an argument that names none is the same for every part.
All inputs are finite; a program needn't handle non-finite values.
Results may differ from a plain program's by a relative error of at most 0.02.
Values are sent between devices in bfloat16 or wider.
A program may use at most 768 MiB of HBM per device.

v0:
```python
import jax
import jax.numpy as jnp
from jax import lax
from jax.sharding import PartitionSpec as P

NAMES = ("w_gate", "w_up", "w_down")


def matmul(a, w):
    return jnp.dot(a, w, preferred_element_type=jnp.float32).astype(jnp.bfloat16)


def normed(h):
    wide = h.astype(jnp.float32)
    scale = lax.rsqrt(jnp.mean(wide**2, -1, keepdims=True) + 1e-6)
    return (wide * scale).astype(jnp.bfloat16)


def layer(h, w):
    a = normed(h)
    gate = jnp.dot(a, w["w_gate"], preferred_element_type=jnp.float32)
    up = jnp.dot(a, w["w_up"], preferred_element_type=jnp.float32)
    return h + matmul((jax.nn.silu(gate) * up).astype(jnp.bfloat16), w["w_down"])


def adamw(w, m, v, g):
    m = 0.9 * m + 0.1 * g
    v = 0.95 * v + 0.05 * g * g
    step = m * lax.rsqrt(v + 1e-8) + 0.1 * w
    return (w - 0.02 * step).astype(jnp.bfloat16), m, v


def solution(mesh):
    def step(x, dy, *arrays):
        weights, m, v = (arrays[i : i + 3] for i in (0, 3, 6))
        layers = weights[0].shape[0]
        h, kept = x[0], []
        for number in range(layers):
            kept.append(h)
            h = layer(h, {name: w[number] for name, w in zip(NAMES, weights, strict=True)})
        by_h, summed = dy[0], [None] * layers
        for number in reversed(range(layers)):
            _, back = jax.vjp(lambda w, h: layer(h, w), {name: w[number] for name, w in zip(NAMES, weights, strict=True)}, kept[number])
            by_w, by_h = back(by_h)
            summed[number] = [lax.psum(by_w[name], "dp") for name in NAMES]
        gradients = [jnp.stack([summed[number][i] for number in range(layers)]).astype(jnp.float32) for i in range(3)]
        new = [adamw(w.astype(jnp.float32), m, v, g) for w, m, v, g in zip(weights, m, v, gradients, strict=True)]
        return tuple(one[which] for which in range(3) for one in new)

    return jax.shard_map(
        step,
        mesh=mesh,
        in_specs=(P(("rep", "dp"), None, None),) * 2 + (P(None, None, None),) * 9,
        out_specs=(P("rep", None, None),) * 9,
        check_vma=False,
    )
```

profile of v0, /device:TPU:97, one launch (start us, length us, event | category | flops | bytes accessed | tf_op | source)
XLA Modules:
  0.0 879.2 jit_solution(10102782665454770736)
XLA Ops:
  7.2 0.1 all-reduce.3.cloned.1.call-start
  7.3 6.5 copy.20
  13.7 3.1 fusion.30
  16.8 0.0 copy-start.8
  16.8 6.5 copy.21
  23.4 0.0 copy-start.5
  23.4 18.3 %convolution_convert_fusion.1 = bf16[2048,2816]{1,0:T(8,128)(2,1)} fusion(bf16[2,2816,1024]{2,1,0:T(8,128)(2,1)} %param.15, bf16[1,2048,1024]{2,1,0:T(8,128)(2,1)} %param.12), kind=kOutput, calls=%fused_computation.59 | convolution fusion | flops 11816927232 | bytes 21495808 | tf_op jit(solution)/shard_map/transpose(jvp())/dot_general | solution.py:10
  41.6 0.0 copy-done.5
  41.6 18.3 %fusion.50 = f32[2048,2816]{1,0:T(8,128)} fusion(bf16[2,1024,2816]{2,1,0:T(8,128)(2,1)} %param.13, bf16[1,2048,1024]{2,1,0:T(8,128)(2,1)S(1)} %copy-done.5, f32[2048]{0:T(1024)S(1)} %add_rsqrt_fusion), kind=kOutput, calls=%fused_computation.84 | convolution fusion | flops 11817451520 | bytes 33038336 | tf_op jit(solution)/shard_map/dot_general | solution.py:21
  59.9 0.0 copy-done.8
  59.9 28.7 %multiply_convert_fusion.1 = (bf16[2048,2816]{1,0:T(8,128)(2,1)}, f32[2048,2816]{1,0:T(8,128)}) fusion(f32[2048,2816]{1,0:T(8,128)} %fusion.50, bf16[2,1024,2816]{2,1,0:T(8,128)(2,1)} %param.14, bf16[1,2048,1024]{2,1,0:T(8,128)(2,1)} %param.11, f32[2048]{0:T(1024)S(1)} %add_rsqrt_fusion), kind=kOutput, calls=%fused_computation.44 | convolution fusion | flops 11852054528 | bytes 67641344 | tf_op jit(solution)/shard_map/dot_general | solution.py:22
  88.6 19.6 %fusion.34 = (f32[2048]{0:T(1024)S(1)}, bf16[2048,1024]{0,1:T(8,128)(2,1)}) fusion(bf16[2048,2816]{1,0:T(8,128)(2,1)} %get-tuple-element.24, bf16[2,2816,1024]{2,1,0:T(8,128)(2,1)} %param.15, bf16[1,2048,1024]{1,2,0:T(8,128)(2,1)} %copy.20), kind=kOutput, calls=%fused_computation.67 | convolution fusion | flops 11821643776 | bytes 25698304 | tf_op jit(solution)/shard_map/dot_general | solution.py:10
  108.2 0.0 copy-start.6
  108.2 0.6 copy-done.6
  108.8 0.0 copy-start.2
  108.8 20.3 %fusion.37 = f32[2048,2816]{1,0:T(8,128)} fusion(bf16[2,1024,2816]{2,1,0:T(8,128)(2,1)} %param.14, bf16[2048,1024]{0,1:T(8,128)(2,1)} %get-tuple-element.27, f32[2048]{0:T(1024)S(1)} %fusion.80), kind=kOutput, calls=%fused_computation.71 | convolution fusion | flops 11817451520 | bytes 33038336 | tf_op jit(solution)/shard_map/jvp()/dot_general | solution.py:22
  129.1 0.0 copy-done.2
  129.1 31.5 %fusion.14 = (bf16[2048,2816]{1,0:T(8,128)(2,1)}, f32[2048,2816]{1,0:T(8,128)}) fusion(f32[2048,2816]{1,0:T(8,128)} %fusion.37, bf16[2048,2816]{1,0:T(8,128)(2,1)} %convolution_convert_fusion.1, bf16[2,1024,2816]{2,1,0:T(8,128)(2,1)} %param.13, bf16[2048,1024]{0,1:T(8,128)(2,1)S(1)} %copy-done.2, f32[2048]{0:T(1024)S(1)} %fusion.80), kind=kOutput, calls=%fused_computation.32 | convolution fusion | flops 11886657536 | bytes 79175680 | tf_op jit(solution)/shard_map/jvp()/dot_general | solution.py:21
  160.6 20.2 %fusion.27 = bf16[2048,1024]{0,1:T(8,128)(2,1)} fusion(bf16[2048,2816]{1,0:T(8,128)(2,1)} %convolution_convert_fusion.1, bf16[2,1024,2816]{2,1,0:T(8,128)(2,1)} %param.14, f32[2048,2816]{1,0:T(8,128)} %get-tuple-element.29), kind=kOutput, calls=%fused_computation.48 | convolution fusion | flops 11845763072 | bytes 44564480 | tf_op jit(solution)/shard_map/transpose(jvp())/dot_general | solution.py:22
  180.8 22.3 %convert_bitcast_fusion.2 = bf16[1,1024,2816]{2,1,0:T(8,128)(2,1)} fusion(bf16[2048,2816]{1,0:T(8,128)(2,1)} %convolution_convert_fusion.1, bf16[2048,1024]{0,1:T(8,128)(2,1)} %get-tuple-element.27, f32[2048]{0:T(1024)S(1)} %fusion.80, f32[2048,2816]{1,0:T(8,128)} %get-tuple-element.29), kind=kOutput, calls=%fused_computation.88 | convolution fusion | flops 11854938112 | bytes 44572672 | tf_op jit(solution)/shard_map/transpose(jvp())/dot_general | solution.py:22
  203.2 0.0 copy-start.3
  203.2 24.0 %convert_bitcast_fusion = bf16[1,2816,1024]{2,1,0:T(8,128)(2,1)} fusion(f32[2048,2816]{1,0:T(8,128)} %fusion.37, bf16[1,2048,1024]{2,1,0:T(8,128)(2,1)} %param.12, f32[2048,2816]{1,0:T(8,128)} %get-tuple-element.29), kind=kOutput, calls=%fused_computation.86 | convolution fusion | flops 11848646656 | bytes 56098816 | tf_op jit(solution)/shard_map/transpose(jvp())/dot_general | solution.py:10
  227.2 0.0 copy-done.3
  227.2 17.5 %convert_bitcast_fusion.4 = bf16[1,1024,2816]{2,1,0:T(8,128)(2,1)} fusion(bf16[2048,2816]{1,0:T(8,128)(2,1)} %get-tuple-element.28, bf16[2048,1024]{0,1:T(8,128)(2,1)S(1)} %copy-done.3, f32[2048]{0:T(1024)S(1)} %fusion.80), kind=kOutput, calls=%fused_computation.90 | convolution fusion | flops 11817451520 | bytes 21504000 | tf_op jit(solution)/shard_map/transpose(jvp())/dot_general | solution.py:21
  244.7 0.0 copy-start.7
  244.7 0.0 copy-start
  244.7 19.2 %fusion.36 = (f32[2048]{0:T(1024)S(1)}, bf16[2048,1024]{0,1:T(8,128)(2,1)}) fusion(bf16[2048,1024]{0,1:T(8,128)(2,1)S(1)} %copy-done.3, bf16[2048,1024]{0,1:T(8,128)(2,1)} %fusion.27, bf16[2048,2816]{1,0:T(8,128)(2,1)} %get-tuple-element.28, bf16[2,1024,2816]{2,1,0:T(8,128)(2,1)} %param.13), kind=kOutput, calls=%fused_computation.69 | convolution fusion | flops 11821643776 | bytes 29892608 | tf_op jit(solution)/shard_map/transpose(jvp())/dot_general | solution.py:21
  264.0 0.0 copy-done.7
  264.0 0.0 copy-done
  264.0 6.0 fusion.64
  270.1 0.0 copy-start.4
  270.1 18.4 %convolution_convert_fusion = bf16[2048,2816]{1,0:T(8,128)(2,1)} fusion(bf16[2048,1024]{0,1:T(8,128)(2,1)} %fusion.64, bf16[2,2816,1024]{2,1,0:T(8,128)(2,1)} %param.15), kind=kOutput, calls=%fused_computation.58 | convolution fusion | flops 11816927232 | bytes 21495808 | tf_op jit(solution)/shard_map/transpose(jvp())/dot_general | solution.py:10
  288.4 0.0 copy-done.4
  288.4 0.0 copy-start.9
  288.4 17.0 %convert_bitcast_fusion.1 = bf16[1,2816,1024]{2,1,0:T(8,128)(2,1)} fusion(bf16[2048,2816]{1,0:T(8,128)(2,1)} %get-tuple-element.24, bf16[2048,1024]{0,1:T(8,128)(2,1)S(1)} %copy-done.4), kind=kOutput, calls=%fused_computation.87 | convolution fusion | flops 11814043648 | bytes 21495808 | tf_op jit(solution)/shard_map/transpose(jvp())/dot_general | solution.py:10
  305.4 0.0 copy-done.9
  305.4 22.3 %convert_bitcast_fusion.3 = bf16[1,1024,2816]{2,1,0:T(8,128)(2,1)} fusion(bf16[2048,2816]{1,0:T(8,128)(2,1)} %convolution_convert_fusion, f32[2048,2816]{1,0:T(8,128)} %fusion.50, bf16[1,2048,1024]{1,2,0:T(8,128)(2,1)} %copy.20, f32[2048]{0:T(1024)S(1)} %copy-done.9), kind=kOutput, calls=%fused_computation.89 | convolution fusion | flops 11854938112 | bytes 44572672 | tf_op jit(solution)/shard_map/transpose(jvp())/dot_general | solution.py:22
  327.8 26.8 %convert_bitcast_fusion.5 = bf16[1,1024,2816]{2,1,0:T(8,128)(2,1)} fusion(f32[2048,2816]{1,0:T(8,128)} %fusion.50, f32[2048,2816]{1,0:T(8,128)} %get-tuple-element.25, bf16[2048,2816]{1,0:T(8,128)(2,1)} %convolution_convert_fusion, bf16[1,2048,1024]{1,2,0:T(8,128)(2,1)} %copy.20, f32[2048]{0:T(1024)S(1)} %copy-done.9), kind=kOutput, calls=%fused_computation.91 | convolution fusion | flops 11883773952 | bytes 67641344 | tf_op jit(solution)/shard_map/transpose(jvp())/dot_general | solution.py:21
  354.5 0.1 all-reduce.3.cloned.1.call-update
  354.6 393.8 %all-reduce.3.cloned.1.call-done = (bf16[1,1024,2816]{2,1,0:T(8,128)(2,1)}, bf16[1,1024,2816]{2,1,0:T(8,128)(2,1)}, bf16[1,1024,2816]{2,1,0:T(8,128)(2,1)}, bf16...) async-done(((bf16[1,1024,2816]{2,1,0:T(8,128)(2,1)}, bf16[1,1024,2816]{2,1,0:T(8,128)(2,1)}, ...) | async-done | bytes 34603024 | tf_op jit(solution)/shard_map/psum | solution.py:45
  748.4 0.0 copy-start.1
  748.4 40.8 %fusion.11 = (bf16[2,2816,1024]{2,1,0:T(8,128)(2,1)}, f32[2,2816,1024]{2,1,0:T(8,128)}, f32[2,2816,1024]{2,1,0:T(8,128)}) fusion(bf16[2,2816,1024]{2,1,0:T(8,128)(2,1)} %param.15, bf16[1,2816,1024]{2,1,0:T(8,128)(2,1)} %get-tuple-element.13, bf16[1,2816,1024]{2,1,0:T(8,128)(2,1)} %get-tuple-element.14, f32[2,2816,1024]{2,1,0:T(8,128)} %param.21, ...), kind=kLoop, calls=%fused_computation.29 | loop fusion | flops 109576192 | bytes 126877696 | tf_op jit(solution)/shard_map/convert_element_type | solution.py:30
  789.2 0.0 copy-done.1
  789.2 82.7 %fusion.2 = (bf16[2,1024,2816]{2,1,0:T(8,128)(2,1)}, f32[2,1024,2816]{2,1,0:T(8,128)}, f32[2,1024,2816]{2,1,0:T(8,128)}, bf16[2,1024,2816]{2,1,0:T(8,128)(2,1)},...) fusion(bf16[2,1024,2816]{2,1,0:T(8,128)(2,1)} %param.13, bf16[1,1024,2816]{2,1,0:T(8,128)(2,1)S(1)} %copy-done.1, ...), kind=kLoop, calls=%fused_computation.20 | loop fusion | flops 219152384 | bytes 253755392 | tf_op jit(solution)/shard_map/convert_element_type | solution.py:30
  (3 shorter events, 0.0 us)
Async XLA Ops:
  7.2 741.2 %all-reduce.3.cloned.1.call-start = ((), (), s32[]{:S(2)}) async-start(), calls=%async_computation | async-start | bytes 69206016 | tf_op jit(solution)/shard_map/psum | solution.py:45
  16.8 43.1 %copy-start.8 = (f32[2048]{0:T(1024)}, f32[2048]{0:T(1024)S(1)}, u32[]{:S(2)}) copy-start(f32[2048]{0:T(1024)S(1)} %add_rsqrt_fusion) | copy-start | bytes 24580
  23.4 18.3 %copy-start.5 = (bf16[1,2048,1024]{2,1,0:T(8,128)(2,1)S(1)}, bf16[1,2048,1024]{2,1,0:T(8,128)(2,1)}, u32[]{:S(2)}) copy-start(bf16[1,2048,1024]{2,1,0:T(8,128)(2,1)} %param.11) | copy-start | bytes 12582916
  108.2 0.6 copy-start.6
  108.8 20.3 %copy-start.2 = (bf16[2048,1024]{0,1:T(8,128)(2,1)S(1)}, bf16[2048,1024]{0,1:T(8,128)(2,1)}, u32[]{:S(2)}) copy-start(bf16[2048,1024]{0,1:T(8,128)(2,1)} %get-tuple-element.27) | copy-start | bytes 12582916
  203.2 24.0 %copy-start.3 = (bf16[2048,1024]{0,1:T(8,128)(2,1)S(1)}, bf16[2048,1024]{0,1:T(8,128)(2,1)}, u32[]{:S(2)}) copy-start(bf16[2048,1024]{0,1:T(8,128)(2,1)} %get-tuple-element.27) | copy-start | bytes 12582916
  244.7 19.2 %copy-start.7 = (f32[2048]{0:T(1024)S(1)}, f32[2048]{0:T(1024)}, u32[]{:S(2)}) copy-start(f32[2048]{0:T(1024)} %copy-done.6) | copy-start | bytes 24580
  244.7 19.3 %copy-start = (bf16[1,2048,1024]{1,2,0:T(8,128)(2,1)S(1)}, bf16[1,2048,1024]{1,2,0:T(8,128)(2,1)}, u32[]{:S(2)}) copy-start(bf16[1,2048,1024]{1,2,0:T(8,128)(2,1)} %copy.21) | copy-start | bytes 12582916
  270.1 18.4 %copy-start.4 = (bf16[2048,1024]{0,1:T(8,128)(2,1)S(1)}, bf16[2048,1024]{0,1:T(8,128)(2,1)}, u32[]{:S(2)}) copy-start(bf16[2048,1024]{0,1:T(8,128)(2,1)} %fusion.64) | copy-start | bytes 12582916
  288.4 17.0 %copy-start.9 = (f32[2048]{0:T(1024)S(1)}, f32[2048]{0:T(1024)}, u32[]{:S(2)}) copy-start(f32[2048]{0:T(1024)} %copy-done.8) | copy-start | bytes 24580
  748.4 40.8 %copy-start.1 = (bf16[1,1024,2816]{2,1,0:T(8,128)(2,1)S(1)}, bf16[1,1024,2816]{2,1,0:T(8,128)(2,1)}, u32[]{:S(2)}) copy-start(bf16[1,1024,2816]{2,1,0:T(8,128)(2,1)} %get-tuple-element.9) | copy-start | bytes 17301508
Sparse Core Ops, SparseCore 0:
  354.7 393.6 all-reduce.2
where the time goes:
time: 888 us; the launch traced here: 879 us
  waiting for transfers between devices  394 us (44%)
  matrix products  324 us (36%)
  other arithmetic  133 us (15%)
  between operations  14.6 us (2%)
  local copies, waits for them, and re-layouts  13.7 us (2%)
    psum x1, waiting for transfers between devices, step(): summed[number] = [lax.psum(by_w[name], 'dp') for name in NAMES]  394 us
    convert_element_type x2, other arithmetic, adamw(): return ((w - 0.02 * step).astype(jnp.bfloat16), m, v)  123 us
    dot_general x5, matrix products, layer(): up = jnp.dot(a, w['w_up'], preferred_element_type=jnp.float32)  114 us
    dot_general x5, matrix products, layer(): gate = jnp.dot(a, w['w_gate'], preferred_element_type=jnp.float32)  113 us
    dot_general x5, matrix products, matmul(): jnp.dot(a, w, preferred_element_type=jnp.float32).astype(jnp.bfloat16)  97.2 us
  transfers between devices with their start and end apart: 1, of which 1 were waited for; matrix products, arithmetic and copies ran while one was open for 0% of the time, Pallas kernels for 0%

commit v1 on v0

v1 whole, which is shorter than its diff:
```python
import functools
import math

import jax
import jax.numpy as jnp
from jax import lax
from jax.experimental import pallas as pl
from jax.experimental.pallas import tpu as pltpu
from jax.sharding import PartitionSpec as P

MESH = pl.DeviceIdType.MESH
F32, BF16 = jnp.float32, jnp.bfloat16
PANELS = 4
LAT = 2
STAGES = 8
G_SLOTS = 2 * LAT + 1
OUT_SLOTS = 4 * LAT + 3
VMEM_LIMIT = 62 * 2**20


def dot(a, b):
    return jnp.dot(a, b, preferred_element_type=F32)


def dot_t(a, b):
    return lax.dot_general(a, b, (((1,), (1,)), ((), ())), preferred_element_type=F32)


def scale_of(wide):
    return lax.rsqrt(jnp.mean(wide**2, -1, keepdims=True) + 1e-6)


def normed(h):
    wide = h.astype(F32)
    return (wide * scale_of(wide)).astype(BF16)


def at_rows(start, size):
    return pl.ds(pl.multiple_of(start, size), size)


def forward_kernel(x_ref, wg_ref, wu_ref, wd_ref, h_ref, x_v, a_v, acc, wgb, wub, wdb, sem, wsem):
    tokens = x_v.shape[0]
    width = wgb.shape[2]
    blocks = wg_ref.shape[2] // width
    tile = min(512, tokens)

    def weights(b, slot):
        cols = at_rows(b * width, width)
        return (
            pltpu.make_async_copy(wg_ref.at[0, :, cols], wgb.at[slot], wsem.at[0, slot]),
            pltpu.make_async_copy(wu_ref.at[0, :, cols], wub.at[slot], wsem.at[1, slot]),
            pltpu.make_async_copy(wd_ref.at[0, cols, :], wdb.at[slot], wsem.at[2, slot]),
        )

    get = pltpu.make_async_copy(x_ref, x_v, sem)
    get.start()
    for c in weights(0, 0):
        c.start()
    get.wait()

    def norm(t, _):
        rows = at_rows(t * tile, tile)
        a_v[rows, :] = normed(x_v[rows, :])
        acc[rows, :] = jnp.zeros((tile, acc.shape[1]), F32)
        return _

    lax.fori_loop(0, tokens // tile, norm, 0)

    def block(b, carry):
        slot = b % 2

        @pl.when(b + 1 < blocks)
        def _next():
            for c in weights(b + 1, 1 - slot):
                c.start()

        for c in weights(b, slot):
            c.wait()

        def part(t, _):
            rows = at_rows(t * tile, tile)
            a = a_v[rows, :]
            gate, up = dot(a, wgb[slot]), dot(a, wub[slot])
            hidden = (jax.nn.silu(gate) * up).astype(BF16)
            acc[rows, :] += dot(hidden, wdb[slot])
            return _

        return lax.fori_loop(0, tokens // tile, part, carry)

    lax.fori_loop(0, blocks, block, 0)

    def out(t, _):
        rows = at_rows(t * tile, tile)
        a_v[rows, :] = x_v[rows, :] + acc[rows, :].astype(BF16)
        return _

    lax.fori_loop(0, tokens // tile, out, 0)
    put = pltpu.make_async_copy(a_v, h_ref, sem)
    put.start()
    put.wait()


def forward(x, wg, wu, wd):
    tokens, d = x.shape
    width = d // PANELS
    hbm = pl.BlockSpec(memory_space=pl.ANY)
    return pl.pallas_call(
        forward_kernel,
        out_shape=jax.ShapeDtypeStruct(x.shape, BF16),
        in_specs=[hbm] * 4,
        out_specs=hbm,
        scratch_shapes=[
            pltpu.VMEM((tokens, d), BF16),
            pltpu.VMEM((tokens, d), BF16),
            pltpu.VMEM((tokens, d), F32),
            pltpu.VMEM((2, d, width), BF16),
            pltpu.VMEM((2, d, width), BF16),
            pltpu.VMEM((2, width, d), BF16),
            pltpu.SemaphoreType.DMA,
            pltpu.SemaphoreType.DMA((3, 2)),
        ],
        compiler_params=pltpu.CompilerParams(vmem_limit_bytes=VMEM_LIMIT),
        cost_estimate=pl.CostEstimate(flops=6 * tokens * d * wg.shape[2], bytes_accessed=2 * (2 * x.size + 3 * d * wg.shape[2]), transcendentals=tokens * wg.shape[2]),
        name="forward",
    )(x, wg, wu, wd)


def backward_kernel(side, x_ref, h_ref, dy_ref, wg_ref, wu_ref, wd_ref, gg_ref, gu_ref, gd_ref,
                    a_v, at_v, ct_v, acc, wgb, wub, wdb, hidt, dgate, dup, own, part1, done,
                    sbuf, rbuf, sem, wsem, osem, ssem, rsem):
    tokens, d = a_v.shape
    panel = wgb.shape[2]
    blocks = wg_ref.shape[2] // panel
    quarter, unit = panel // side, panel // side // side
    tile = min(512, tokens)
    chunks = 2 * blocks * 3
    half = 3 * quarter + 3 * unit
    X1, X2, Y1, Y2 = 0, quarter, 3 * quarter, 3 * quarter + unit
    AY1, AY2, AX1, AX2 = half, half + 2 * unit, half + 3 * unit, half + 3 * unit + 2 * quarter

    rep, me = lax.axis_index("rep"), lax.axis_index("dp")
    px, py = me // side, me % side
    device = lambda x, y: (rep, (x % side) * side + y % side)
    near = (device(px + 1, py), device(px + side - 1, py), device(px, py + 1), device(px, py + side - 1))
    colours = ((0, (0, 1), (2, 3), px, py), (1, (2, 3), (0, 1), py, px))

    barrier = pltpu.get_barrier_semaphore()
    for n in near:
        pl.semaphore_signal(barrier, inc=1, device_id=n, device_id_type=MESH)
    pl.semaphore_wait(barrier, 4)

    def message(link, which, i):
        rows = pl.ds(which * half, half)
        return pltpu.make_async_remote_copy(
            src_ref=sbuf.at[link, i % LAT, rows],
            dst_ref=rbuf.at[link, i % (2 * LAT), rows],
            send_sem=ssem.at[which, link, i % LAT],
            recv_sem=rsem.at[which, link, i % (2 * LAT)],
            device_id=near[link],
            device_id_type=MESH,
        )

    def result(kind, c):
        slot = c % OUT_SLOTS
        number = c // 3
        layer, cols = 1 - number // blocks, at_rows((number % blocks) * panel, panel)
        if kind:
            ref = (gg_ref, gu_ref)[kind - 1]
            return [pltpu.make_async_copy(done.at[slot], ref.at[layer, :, cols], osem.at[slot])]
        return [
            pltpu.make_async_copy(done.at[slot, pl.ds(k * panel, panel)], gd_ref.at[layer, cols, pl.ds(k * panel, panel)], osem.at[slot])
            for k in range(PANELS)
        ]

    def wait_result(c):
        pltpu.make_async_copy(done.at[c % OUT_SLOTS], gg_ref.at[0, :, pl.ds(0, panel)], osem.at[c % OUT_SLOTS]).wait()

    def tick(i, k):
        sent, got = i % LAT, (i + LAT) % (2 * LAT)

        @pl.when((i >= LAT) & (i - LAT < chunks + 3 * LAT))
        def _():
            for link in range(4):
                message(link, 0, i + LAT).wait_send()
                message(link, 0, i + LAT).wait_recv()

        @pl.when((i >= 5 * LAT) & (i - LAT < chunks + 7 * LAT))
        def _():
            for link in range(4):
                message(link, 1, i + LAT).wait_send()
                message(link, 1, i + LAT).wait_recv()

        def stage(s):
            c = i - s * LAT
            return c, pl.when((c >= 0) & (c < chunks))

        def quarter_rows(p, k):
            return at_rows(p * panel + (k % side) * quarter, quarter)

        def unit_rows(p, k, j):
            return at_rows(p * panel + (k % side) * quarter + (j % side) * unit, unit)

        def unit_of(p, j):
            return at_rows(p * quarter + (j % side) * unit, unit)

        wide = lambda v: v.astype(F32)

        c0, when = stage(0)

        @when
        def _():
            for colour, one, two, p, q in colours:
                for j in range(2):
                    sbuf[one[j], sent, pl.ds(X1, quarter)] = own[c0 % G_SLOTS, quarter_rows(2 * colour + j, p + 2)]

        c1, when = stage(1)

        @when
        def _():
            slot = c1 % G_SLOTS
            for colour, one, two, p, q in colours:
                for j in range(2):
                    to = p + (1, side - 1)[j]
                    for w in range(2):
                        v = own[slot, quarter_rows(2 * colour + w, to)]
                        if w == j:
                            v = (wide(v) + wide(rbuf[one[j], got, pl.ds(X1, quarter)])).astype(BF16)
                        sbuf[one[j], sent, pl.ds(X2 + w * quarter, quarter)] = v

        c2, when = stage(2)

        @when
        def _():
            slot = c2 % G_SLOTS
            for colour, one, two, p, q in colours:
                for w in range(2):
                    rows = pl.ds(X2 + w * quarter, quarter)
                    part1[slot, colour, pl.ds(w * quarter, quarter)] = (
                        wide(own[slot, quarter_rows(2 * colour + w, p)]) + wide(rbuf[one[0], got, rows]) + wide(rbuf[one[1], got, rows])
                    )
                for j in range(2):
                    sbuf[two[j], sent, pl.ds(Y1, unit)] = part1[slot, colour, unit_of(j, q + 2)].astype(BF16)

        c3, when = stage(3)

        @when
        def _():
            slot = c3 % G_SLOTS
            for colour, one, two, p, q in colours:
                for j in range(2):
                    to = q + (1, side - 1)[j]
                    for w in range(2):
                        v = part1[slot, colour, unit_of(w, to)]
                        if w == j:
                            v = v + wide(rbuf[two[j], got, pl.ds(Y1, unit)])
                        sbuf[two[j], sent, pl.ds(Y2 + w * unit, unit)] = v.astype(BF16)

        c4, when = stage(4)

        @when
        def _():
            @pl.when(c4 >= OUT_SLOTS)
            def _():
                wait_result(c4)

            slot, to = c4 % G_SLOTS, c4 % OUT_SLOTS
            for colour, one, two, p, q in colours:
                for w in range(2):
                    rows = pl.ds(Y2 + w * unit, unit)
                    v = part1[slot, colour, unit_of(w, q)] + wide(rbuf[two[0], got, rows]) + wide(rbuf[two[1], got, rows])
                    v = v.astype(BF16)
                    done[to, unit_rows(2 * colour + w, p, q)] = v
                    for j in range(2):
                        sbuf[two[j], sent, pl.ds(AY1 + w * unit, unit)] = v

        c5, when = stage(5)

        @when
        def _():
            to = c5 % OUT_SLOTS
            for colour, one, two, p, q in colours:
                for j in range(2):
                    for w in range(2):
                        v = rbuf[two[j], got, pl.ds(AY1 + w * unit, unit)]
                        done[to, unit_rows(2 * colour + w, p, q + (side - 1, 1)[j])] = v
                        if w == j:
                            sbuf[two[j], sent, pl.ds(AY2, unit)] = v

        c6, when = stage(6)

        @when
        def _():
            to = c6 % OUT_SLOTS
            for colour, one, two, p, q in colours:
                for j in range(2):
                    done[to, unit_rows(2 * colour + j, p, q + 2)] = rbuf[two[j], got, pl.ds(AY2, unit)]
                for w in range(2):
                    v = done[to, quarter_rows(2 * colour + w, p)]
                    for j in range(2):
                        sbuf[one[j], sent, pl.ds(AX1 + w * quarter, quarter)] = v

        c7, when = stage(7)

        @when
        def _():
            to = c7 % OUT_SLOTS
            for colour, one, two, p, q in colours:
                for j in range(2):
                    for w in range(2):
                        v = rbuf[one[j], got, pl.ds(AX1 + w * quarter, quarter)]
                        done[to, quarter_rows(2 * colour + w, p + (side - 1, 1)[j])] = v
                        if w == j:
                            sbuf[one[j], sent, pl.ds(AX2, quarter)] = v

        c8, when = stage(8)

        @when
        def _():
            to = c8 % OUT_SLOTS
            for colour, one, two, p, q in colours:
                for j in range(2):
                    done[to, quarter_rows(2 * colour + j, p + 2)] = rbuf[one[j], got, pl.ds(AX2, quarter)]
            for c in result((k - 8 * LAT) % 3, c8):
                c.start()

        @pl.when(i < chunks + 3 * LAT)
        def _():
            for link in range(4):
                message(link, 0, i).start()

        @pl.when((i >= 4 * LAT) & (i < chunks + 7 * LAT))
        def _():
            for link in range(4):
                message(link, 1, i).start()

    def weights(number, slot):
        layer, cols = 1 - number // blocks, at_rows((number % blocks) * panel, panel)
        return (
            pltpu.make_async_copy(wg_ref.at[layer, :, cols], wgb.at[slot], wsem.at[0, slot]),
            pltpu.make_async_copy(wu_ref.at[layer, :, cols], wub.at[slot], wsem.at[1, slot]),
            pltpu.make_async_copy(wd_ref.at[layer, cols, :], wdb.at[slot], wsem.at[2, slot]),
        )

    def take_in(_t, _):
        rows = at_rows(_t * tile, tile)
        a = normed(a_v[rows, :])
        a_v[rows, :] = a
        at_v[:, rows] = a.T
        return _

    for c in weights(0, 0):
        c.start()
    gets = (pltpu.make_async_copy(h_ref, a_v, sem.at[0]), pltpu.make_async_copy(dy_ref, ct_v, sem.at[1]))
    for c in gets:
        c.start()
    for c in gets:
        c.wait()
    lax.fori_loop(0, tokens // tile, take_in, 0)

    def next_layer():
        get = pltpu.make_async_copy(h_ref, a_v, sem.at[0])
        get.start()
        get.wait()
        small = tile // 4

        def back(t, _):
            rows = at_rows(t * small, small)
            wide = a_v[rows, :].astype(F32)
            scale = scale_of(wide)
            by_a = acc[rows, :].astype(BF16).astype(F32)
            inner = jnp.mean(by_a * wide, -1, keepdims=True)
            by_h = by_a * scale - wide * (scale * scale * scale * inner)
            ct_v[rows, :] = ct_v[rows, :] + by_h.astype(BF16)
            return _

        lax.fori_loop(0, tokens // small, back, 0)
        get = pltpu.make_async_copy(x_ref, a_v, sem.at[0])
        get.start()
        get.wait()
        lax.fori_loop(0, tokens // tile, take_in, 0)

    def block(number, carry):
        slot = number % 2
        later = number < blocks

        pl.when(number == blocks)(next_layer)

        for c in weights(number, slot):
            c.wait()

        @pl.when(number + 1 < 2 * blocks)
        def _():
            for c in weights(number + 1, 1 - slot):
                c.start()

        def hidden(t, _):
            rows = at_rows(t * tile, tile)
            a = a_v[rows, :]
            gate, up = dot(a, wgb[slot]), dot(a, wub[slot])
            by_hidden = dot_t(ct_v[rows, :], wdb[slot]).astype(BF16).astype(F32)
            sigmoid = jax.nn.sigmoid(gate)
            silu = gate * sigmoid
            hidt[:, rows] = (silu * up).astype(BF16).T
            dup[rows, :] = (by_hidden * silu).astype(BF16)
            dgate[rows, :] = (by_hidden * up * (sigmoid + silu * (1.0 - sigmoid))).astype(BF16)
            return _

        lax.fori_loop(0, tokens // tile, hidden, 0)

        def into(first, by, w):
            def go(t, _):
                rows = at_rows(t * tile, tile)
                v = dot_t(by[rows, :], w[slot])
                if first:
                    v = jnp.where(number == 0, v, acc[rows, :] + v)
                else:
                    v = acc[rows, :] + v
                acc[rows, :] = v
                return _

            @pl.when(later)
            def _():
                lax.fori_loop(0, tokens // tile, go, 0)

        i = 3 * number
        for k in range(PANELS):
            own[i % G_SLOTS, pl.ds(k * panel, panel)] = dot(hidt[...], ct_v[:, pl.ds(k * panel, panel)]).astype(BF16)
        tick(i, 0)
        for k in range(PANELS):
            own[(i + 1) % G_SLOTS, pl.ds(k * panel, panel)] = dot(at_v[pl.ds(k * panel, panel), :], dgate[...]).astype(BF16)
        into(True, dgate, wgb)
        tick(i + 1, 1)
        for k in range(PANELS):
            own[(i + 2) % G_SLOTS, pl.ds(k * panel, panel)] = dot(at_v[pl.ds(k * panel, panel), :], dup[...]).astype(BF16)
        into(False, dup, wub)
        tick(i + 2, 2)
        return carry

    lax.fori_loop(0, 2 * blocks, block, 0)

    def drain(t, _):
        for k in range(3):
            tick(chunks + 3 * t + k, k)
        return _

    lax.fori_loop(0, (STAGES * LAT + 3) // 3, drain, 0)
    for c in range(chunks - OUT_SLOTS, chunks):
        wait_result(c)


def backward(side, x, h, dy, wg, wu, wd):
    tokens, d = x.shape
    panel = d // PANELS
    rows = 6 * (panel // side + panel // side // side)
    hbm = pl.BlockSpec(memory_space=pl.ANY)
    return pl.pallas_call(
        functools.partial(backward_kernel, side),
        out_shape=tuple(jax.ShapeDtypeStruct(w.shape, BF16) for w in (wg, wu, wd)),
        in_specs=[hbm] * 6,
        out_specs=(hbm,) * 3,
        scratch_shapes=[
            pltpu.VMEM((tokens, d), BF16),
            pltpu.VMEM((d, tokens), BF16),
            pltpu.VMEM((tokens, d), BF16),
            pltpu.VMEM((tokens, d), F32),
            pltpu.VMEM((2, d, panel), BF16),
            pltpu.VMEM((2, d, panel), BF16),
            pltpu.VMEM((2, panel, d), BF16),
            pltpu.VMEM((panel, tokens), BF16),
            pltpu.VMEM((tokens, panel), BF16),
            pltpu.VMEM((tokens, panel), BF16),
            pltpu.VMEM((G_SLOTS, d, panel), BF16),
            pltpu.VMEM((G_SLOTS, 2, 2 * panel // side, panel), F32),
            pltpu.VMEM((OUT_SLOTS, d, panel), BF16),
            pltpu.VMEM((4, LAT, rows, panel), BF16),
            pltpu.VMEM((4, 2 * LAT, rows, panel), BF16),
            pltpu.SemaphoreType.DMA((2,)),
            pltpu.SemaphoreType.DMA((3, 2)),
            pltpu.SemaphoreType.DMA((OUT_SLOTS,)),
            pltpu.SemaphoreType.DMA((2, 4, LAT)),
            pltpu.SemaphoreType.DMA((2, 4, 2 * LAT)),
        ],
        compiler_params=pltpu.CompilerParams(collective_id=0, has_side_effects=True, vmem_limit_bytes=VMEM_LIMIT),
        cost_estimate=pl.CostEstimate(flops=28 * tokens * d * wg.shape[2], bytes_accessed=4 * 3 * wg.size, transcendentals=2 * tokens * wg.shape[2]),
        name="backward",
    )(x, h, dy, wg, wu, wd)


def adamw(w, m, v, g):
    m = 0.9 * m + 0.1 * g
    v = 0.95 * v + 0.05 * g * g
    step = m * lax.rsqrt(v + 1e-8) + 0.1 * w
    return (w - 0.02 * step).astype(BF16), m, v


def solution(mesh):
    side = math.isqrt(mesh.shape["dp"])

    def step(x, dy, *arrays):
        weights, m, v = (arrays[i : i + 3] for i in (0, 3, 6))
        h = forward(x[0], *weights)
        gradients = backward(side, x[0], h, dy[0], *weights)
        new = [adamw(w.astype(F32), m, v, g.astype(F32)) for w, m, v, g in zip(weights, m, v, gradients, strict=True)]
        return tuple(one[which] for which in range(3) for one in new)

    return jax.shard_map(
        step,
        mesh=mesh,
        in_specs=(P(("rep", "dp"), None, None),) * 2 + (P(None, None, None),) * 9,
        out_specs=(P("rep", None, None),) * 9,
        check_vma=False,
    )
```

time: 888 us -> 598 us (0.67)
  Pallas kernels: 0 us -> 469 us
  waiting for transfers between devices: 394 us -> 0 us
  matrix products: 324 us -> 0 us
  between operations: 14.6 us -> 0.66 us
  local copies, waits for them, and re-layouts: 13.7 us -> 0 us
    pallas_call x0 -> x2, Pallas kernels: none -> 469 us  [the longest x1 418 us: backward(): pl.pallas_call(functools.partial(backward_kernel, side), out_shape=tuple(...]
    psum x1 -> x0, waiting for transfers between devices: 394 us -> none  [step(): summed[number] = [lax.psum(by_w[name], 'dp') for name in NAMES]]
    dot_general x15 -> x0, matrix products: 324 us -> none  [the longest x5 114 us: layer(): up = jnp.dot(a, w['w_up'], preferred_element_type=jnp.float32)]
    unnamed x22 -> x0, local copies, waits for them, and re-layouts: 13.7 us -> none
  transfers between devices with their start and end apart: 1 -> 0, of which waited for: 1 -> 0; matrix products, arithmetic and copies ran while one was open for 0% -> 0% of each run, Pallas kernels for 0% -> 0%
where the time goes in v1:
time: 598 us; the launch traced here: 594 us
  Pallas kernels  469 us (78%)
  other arithmetic  125 us (21%)
    pallas_call x1, Pallas kernels, backward(): pl.pallas_call(functools.partial(backward_kernel, side), out_shape=tuple(...  418 us
    convert_element_type x2, other arithmetic, adamw(): return ((w - 0.02 * step).astype(BF16), m, v)  125 us
    pallas_call x1, Pallas kernels, forward(): pl.pallas_call(forward_kernel, out_shape=jax.ShapeDtypeStruct(x.shape, BF...  50.4 us

profile of v1, /device:TPU:97, one launch (start us, length us, event | category | flops | bytes accessed | tf_op | source)
XLA Modules:
  0.0 593.9 jit_solution(9753797121227895397)
XLA Ops:
  0.6 50.4 %forward.1.h_ref = bf16[2048,1024]{1,0:T(8,128)(2,1)} custom-call(bf16[2048,1024]{1,0:T(8,128)(2,1)} %bitcast.2, bf16[2,1024,2816]{2,1,0:T(8,128)(2,1)} %wg_ref.3, bf16[2,1024,2816]{2,1,0:T(8,128)(2,1)} %wu_ref.3, bf16[2,2816,1024]{2,1,0:T(8,128)(2,1)} %wd_ref.3), custom_call_target="tpu_custom_call" | custom-call | flops 35433480192 | bytes 25690112 | tf_op jit(solution)/shard_map/forward/pallas_call | solution.py:108
  51.1 418.1 %backward.1 = (bf16[2,1024,2816]{2,1,0:T(8,128)(2,1)}, bf16[2,1024,2816]{2,1,0:T(8,128)(2,1)}, bf16[2,2816,1024]{2,1,0:T(8,128)(2,1)}) custom-call(bf16[2048,1024]{1,0:T(8,128)(2,1)} %bitcast.3, bf16[2048,1024]{1,0:T(8,128)(2,1)} %forward.1.h_ref, bf16[2048,1024]{1,0:T(8,128)(2,1)} %bitcast.4, bf16[2,1024,2816]{2,1,0:T(8,128)(2,1)} %wg_ref.3, ...), custom_call_target="tpu_custom_call" | custom-call | flops 165356240896 | bytes 69206016 | tf_op jit(solution)/shard_map/backward/pallas_call | solution.py:457
  469.2 84.5 %fusion.2 = (bf16[2,1024,2816]{2,1,0:T(8,128)(2,1)}, f32[2,1024,2816]{2,1,0:T(8,128)}, f32[2,1024,2816]{2,1,0:T(8,128)}, bf16[2,1024,2816]{2,1,0:T(8,128)(2,1)},...) fusion(bf16[2,1024,2816]{2,1,0:T(8,128)(2,1)} %wg_ref.3, bf16[2,1024,2816]{2,1,0:T(8,128)(2,1)} %get-tuple-element.12, ...), kind=kLoop, calls=%fused_computation.14 | loop fusion | flops 184549376 | bytes 253755392 | tf_op jit(solution)/shard_map/convert_element_type | solution.py:494
  553.7 40.2 %fusion.10 = (bf16[2,2816,1024]{2,1,0:T(8,128)(2,1)}, f32[2,2816,1024]{2,1,0:T(8,128)}, f32[2,2816,1024]{2,1,0:T(8,128)}) fusion(bf16[2,2816,1024]{2,1,0:T(8,128)(2,1)} %wd_ref.3, bf16[2,2816,1024]{2,1,0:T(8,128)(2,1)} %get-tuple-element.14, f32[2,2816,1024]{2,1,0:T(8,128)} %param.21, f32[2,2816,1024]{2,1,0:T(8,128)} %param.18), kind=kLoop, calls=%fused_computation.22 | loop fusion | flops 92274688 | bytes 126877696 | tf_op jit(solution)/shard_map/convert_element_type | solution.py:494
